TPU v7x, 512 devices: a whole 4x4x16 slice. The times are simulated.
512 devices in a mesh: seq: 64 (over z, x), head: 8 (over y, core).
Axes of the slice: x: 4, y: 4, z: 16, core: 2. Of those that a mesh axis runs over, the one named last changes fastest.
Arguments:
- x_proj: bfloat16 [16384, 8192], P(('seq', 'head')), may hold values from -6 to 6
- z_proj: bfloat16 [16384, 8192], P(('seq', 'head')), may hold values from -6 to 6
- b_proj: bfloat16 [16384, 1024], P(('seq', 'head')), may hold values from -6 to 6
- c_proj: bfloat16 [16384, 1024], P(('seq', 'head')), may hold values from -6 to 6
- dt_raw: bfloat16 [16384, 128], P(('seq', 'head')), may hold values from -3.2 to 3.2, as said below
- dt_bias: float32 [128], P('head'), may hold values from -6.3 to -1.2, as said below
- a_log: float32 [128], P('head'), as said below
- d_skip: float32 [128], P('head'), may hold values from 0.5 to 2
- conv_x: float32 [4, 8192], P(None, 'head'), may hold values from -3 to 3
- conv_bias_x: float32 [8192], P('head'), may hold values from -3 to 3
- conv_bc: float32 [4, 2, 1024], P(None, None, 'head'), may hold values from -3 to 3
- conv_bias_bc: float32 [2, 1024], P(None, 'head'), may hold values from -3 to 3
- norm_weight: float32 [8192], P('head'), may hold values from 0.25 to 1.75
- out_weight: bfloat16 [8192, 4096], P('head', 'seq'), may hold values from -0.0625 to 0.0625
Outputs:
- mixed: bfloat16 [16384, 4096], P(('seq', 'head'))
Inputs may be any that keep to these rules, and one draw needn't show every extreme that they name: `dt_raw`: A normal draw times 0.7 plus an offset common to each head and each aligned run of 256 tokens. `dt_bias`: the inverse softplus of a per-head step size between 0.002 and 0.25. Finite; exp(a_log) lies above 0.0 and at most 0.3.
All inputs are finite; a program needn't handle non-finite values.
Results may differ from a plain program's by a relative error of at most 0.014.
Values may be sent and summed in bfloat16 or wider, within the bound.
No kernel may reach another device: no remote copies, remote signals or barrier semaphores. Data moves between devices by JAX's collectives and lax.ppermute only.
A program may use at most 128 MiB of HBM per device.

v0:
```python
import jax
import jax.numpy as jnp
from jax import lax
from jax.sharding import Mesh
from jax.sharding import PartitionSpec as P

HEAD_DIM = 64
STATE = 128
GROUPS = 8
SPAN = 128
DI = 8192
SEQ = ("seq_0", "seq_1")
SEQ_HEAD = ("seq_0", "seq_1", "head")


def from_behind(array, axis, by):
    count = lax.axis_size(axis)
    pairs = [(i, i + by) for i in range(count) if 0 <= i + by < count]
    return lax.ppermute(array, axis, pairs)


def filled_with(array, identity):
    return jax.tree.map(
        lambda a, e: jnp.broadcast_to(jnp.asarray(e, a.dtype), a.shape), array, identity
    )


def entering(array, axes, combine, identity):
    before = start = filled_with(array, identity)
    total = array
    for axis in reversed(axes):
        count, mine = (lax.axis_size(axis), lax.axis_index(axis))
        pieces = jax.tree.map(lambda part: lax.all_gather(part, axis), total)
        inside, total = (start, start)
        for k in range(count):
            passed = k < mine
            total = combine(total, jax.tree.map(lambda part: part[k], pieces))
            inside = jax.tree.map(lambda new, old: jnp.where(passed, new, old), total, inside)
        before = combine(inside, before)
    return before


def split_up(array, dim, count):
    shape = array.shape
    pieces = array.reshape(*shape[:dim], count, shape[dim] // count, *shape[dim + 1 :])
    return jnp.moveaxis(pieces, dim, 0)


def sent_and_summed(array, axis, dim):
    count = lax.axis_size(axis)
    pieces = lax.all_to_all(split_up(array, dim, count), axis, 0, 0, tiled=True)
    return jnp.sum(pieces.astype(jnp.float32), axis=0)


def depthwise(current, previous, weight, bias_row):
    padded = jnp.concatenate([previous, current], axis=0).astype(jnp.float32)
    token_count = current.shape[0]
    summed = jnp.broadcast_to(bias_row, current.shape)
    for offset in range(weight.shape[0]):
        summed = summed + weight[offset] * padded[offset : offset + token_count]
    return jax.nn.silu(summed).astype(jnp.bfloat16)


def block_weights(c_blocks, b_blocks, cumulative, step_size, per_group):
    scores = jnp.einsum("ktgn,ksgn->kgts", c_blocks, b_blocks, preferred_element_type=jnp.float32)
    by_head = jnp.transpose(cumulative, (0, 2, 1))
    spread = by_head[:, :, :, None] - by_head[:, :, None, :]
    length = cumulative.shape[1]
    causal = jnp.arange(length)[:, None] >= jnp.arange(length)[None, :]
    decays = jnp.exp(jnp.where(causal, spread, -jnp.inf))
    scaled = decays * jnp.transpose(step_size, (0, 2, 1))[:, :, None, :]
    block_count = cumulative.shape[0]
    head_count = cumulative.shape[2]
    grouped = scaled.reshape(block_count, -1, per_group, length, length) * scores[:, :, None]
    return grouped.reshape(block_count, head_count, length, length).astype(jnp.bfloat16)


def combine_states(earlier, later):
    return (earlier[0] + later[0], jnp.exp(later[0])[:, None, None] * earlier[1] + later[1])


def per_device(
    x_proj,
    z_proj,
    b_proj,
    c_proj,
    dt_raw,
    dt_bias,
    a_log,
    d_skip,
    conv_x,
    conv_bias_x,
    conv_bc,
    conv_bias_bc,
    norm_weight,
    out_weight,
):
    x_heads, z_heads, b_heads, c_heads, dt_heads = (
        lax.all_to_all(x_proj, "head", split_axis=1, concat_axis=0, tiled=True),
        lax.all_to_all(z_proj, "head", split_axis=1, concat_axis=0, tiled=True),
        lax.all_to_all(b_proj, "head", split_axis=1, concat_axis=0, tiled=True),
        lax.all_to_all(c_proj, "head", split_axis=1, concat_axis=0, tiled=True),
        lax.all_to_all(dt_raw, "head", split_axis=1, concat_axis=0, tiled=True),
    )
    kernel_len = conv_x.shape[0]
    x_cols = x_heads.shape[1]
    bc_cols = b_heads.shape[1]
    last_rows = jnp.concatenate(
        [x_heads[-(kernel_len - 1) :], b_heads[-(kernel_len - 1) :], c_heads[-(kernel_len - 1) :]],
        axis=1,
    )
    before = from_behind(last_rows, SEQ, 1)
    x_conv = depthwise(x_heads, before[:, :x_cols], conv_x, conv_bias_x)
    b_conv = depthwise(
        b_heads, before[:, x_cols : x_cols + bc_cols], conv_bc[:, 0], conv_bias_bc[0]
    )
    c_conv = depthwise(c_heads, before[:, x_cols + bc_cols :], conv_bc[:, 1], conv_bias_bc[1])
    token_count = x_conv.shape[0]
    local_heads = dt_bias.shape[0]
    local_groups = bc_cols // STATE
    per_group = local_heads // local_groups
    blocks = token_count // SPAN
    x_blocks = x_conv.reshape(blocks, SPAN, local_heads, HEAD_DIM)
    b_blocks = b_conv.reshape(blocks, SPAN, local_groups, STATE)
    c_blocks = c_conv.reshape(blocks, SPAN, local_groups, STATE)
    step_size = jax.nn.softplus(dt_heads.astype(jnp.float32) + dt_bias).reshape(
        blocks, SPAN, local_heads
    )
    cumulative = jnp.cumsum(-jnp.exp(a_log) * step_size, axis=1)
    mix_weights = block_weights(c_blocks, b_blocks, cumulative, step_size, per_group)
    y_local = jnp.einsum(
        "khts,kshp->kthp", mix_weights, x_blocks, preferred_element_type=jnp.float32
    )
    state_scale = step_size * jnp.exp(cumulative[:, -1:, :] - cumulative)
    x_weighted = (x_blocks.astype(jnp.float32) * state_scale[:, :, :, None]).astype(jnp.bfloat16)
    x_grouped = x_weighted.reshape(blocks, SPAN, local_groups, per_group, HEAD_DIM)
    pieces = jnp.einsum(
        "ksgqp,ksgn->kgqpn", x_grouped, b_blocks, preferred_element_type=jnp.float32
    )
    pieces = pieces.reshape(blocks, local_heads, HEAD_DIM, STATE)
    totals = cumulative[:, -1, :]
    final_state = jnp.zeros((local_heads, HEAD_DIM, STATE), jnp.float32)
    for block_idx in range(blocks):
        final_state = jnp.exp(totals[block_idx])[:, None, None] * final_state + pieces[block_idx]
    log_total = jnp.sum(totals, axis=0)
    carried = entering(
        (log_total, final_state),
        SEQ,
        combine_states,
        (jnp.zeros_like(log_total), jnp.zeros_like(final_state)),
    )
    running = carried[1]
    start_list = []
    for block_idx in range(blocks):
        start_list.append(running.astype(jnp.bfloat16))
        running = jnp.exp(totals[block_idx])[:, None, None] * running + pieces[block_idx]
    start_states = jnp.stack(start_list).reshape(blocks, local_groups, per_group, HEAD_DIM, STATE)
    y_carry = jnp.einsum(
        "ktgn,kgqpn->ktgqp", c_blocks, start_states, preferred_element_type=jnp.float32
    )
    y_carry = (
        y_carry.reshape(blocks, SPAN, local_heads, HEAD_DIM) * jnp.exp(cumulative)[:, :, :, None]
    )
    outputs = y_local + y_carry + d_skip[:, None] * x_blocks.astype(jnp.float32)
    outputs = outputs.reshape(token_count, local_heads * HEAD_DIM)
    gated = outputs * jax.nn.silu(z_heads.astype(jnp.float32))
    grouped = gated.reshape(token_count, -1, DI // GROUPS)
    normed = grouped / jnp.sqrt(jnp.mean(grouped * grouped, axis=-1, keepdims=True) + 1.0)
    normed = (normed.reshape(token_count, -1) * norm_weight).astype(jnp.bfloat16)
    terms = jnp.dot(
        normed,
        lax.all_gather(out_weight, SEQ, axis=1, tiled=True),
        preferred_element_type=jnp.float32,
    )
    mixed = sent_and_summed(terms.astype(jnp.bfloat16), "head", 0)
    return mixed.astype(jnp.bfloat16)


def solution(mesh):
    split = Mesh(mesh.devices.reshape(16, 4, mesh.shape["head"]), ("seq_0", "seq_1", "head"))
    return jax.shard_map(
        per_device,
        mesh=split,
        in_specs=(
            P(SEQ_HEAD, None),
            P(SEQ_HEAD, None),
            P(SEQ_HEAD, None),
            P(SEQ_HEAD, None),
            P(SEQ_HEAD, None),
            P("head"),
            P("head"),
            P("head"),
            P(None, "head"),
            P("head"),
            P(None, None, "head"),
            P(None, "head"),
            P("head"),
            P("head", SEQ),
        ),
        out_specs=P(SEQ_HEAD, None),
        check_vma=False,
    )
```

profile of v0, /device:TPU:1, one launch (start us, length us, event | category | flops | bytes accessed | tf_op | source)
XLA Modules:
  0.0 415.9 jit_solution(11446474946781498572)
XLA Ops:
  6.5 0.8 copy.58
  7.4 0.7 reshape.437
  8.1 10.0 %all-to-all-start.3 = ((bf16[8,2,256]{2,1,0:T(2,128)(2,1)}), bf16[8,2,256]{2,1,0:T(2,128)(2,1)S(1)}, u32[]{:S(2)}, u32[]{:S(2)}) async-start(bf16[8,2,256]{2,1,0:T(2,128)(2,1)} %reshape.437), calls=%async_computation.3 | async-start | bytes 16384 | tf_op jit(solution)/shard_map/all_to_all | solution.py:103
  18.1 0.6 copy_bitcast_fusion.3
  18.7 1.5 copy_bitcast_fusion.2
  20.2 1.4 slice_bitcast_fusion.3
  21.6 1.3 slice_bitcast_fusion.4
  22.9 0.9 fusion.62
  23.8 0.7 exponential_negate_fusion
  24.4 1.9 copy.87
  26.3 4.8 %all-to-all-start.1 = ((bf16[32,8,128]{2,0,1:T(8,128)(2,1)}), bf16[32,8,128]{2,0,1:T(8,128)(2,1)S(1)}, u32[]{:S(2)}, u32[]{:S(2)}) async-start(bf16[32,8,128]{2,0,1:T(8,128)(2,1)} %copy_bitcast_fusion.3), calls=%async_computation.1 | async-start | bytes 131072 | tf_op jit(solution)/shard_map/all_to_all | solution.py:101
  31.1 0.1 reshape.438
  31.2 0.1 copy.59
  31.3 0.8 broadcast_multiply_fusion
  32.1 0.2 reduce_window_sum.11
  32.3 3.7 all-to-all-done.1
  36.0 4.0 all-to-all-start.2
  40.0 4.8 %all-to-all-done.2 = bf16[32,8,128]{2,0,1:T(8,128)(2,1)S(1)} async-done(((bf16[32,8,128]{2,0,1:T(8,128)(2,1)}), bf16[32,8,128]{2,0,1:T(8,128)(2,1)S(1)}, u32[]{:S(2)}, u32[]{:S(2)}) %all-to-all-start.2) | async-done | bytes 65568 | tf_op jit(solution)/shard_map/all_to_all | solution.py:102
  44.9 4.2 %all-to-all-start = ((bf16[32,8,1024]{2,0,1:T(8,128)(2,1)}), bf16[32,8,1024]{2,0,1:T(8,128)(2,1)S(1)}, u32[]{:S(2)}, u32[]{:S(2)}) async-start(bf16[32,8,1024]{2,0,1:T(8,128)(2,1)} %bitcast.167), calls=%async_computation | async-start | bytes 1048576 | tf_op jit(solution)/shard_map/all_to_all | solution.py:99
  49.1 0.5 fusion.36
  49.6 0.1 exponential_multiply_fusion
  49.7 8.7 %all-to-all-done = bf16[32,8,1024]{2,0,1:T(8,128)(2,1)S(1)} async-done(((bf16[32,8,1024]{2,0,1:T(8,128)(2,1)}), bf16[32,8,1024]{2,0,1:T(8,128)(2,1)S(1)}, u32[]{:S(2)}, u32[]{:S(2)}) %all-to-all-start) | async-done | bytes 524320 | tf_op jit(solution)/shard_map/all_to_all | solution.py:99
  58.5 1.3 collective-permute-start
  59.8 0.7 collective-permute-done
  60.6 0.1 maximum_convert_fusion
  60.7 0.7 multiply_convert_fusion.3
  61.4 0.7 reshape.436
  62.1 0.9 copy.63
  63.0 0.1 multiply_convert_fusion.4
  63.1 0.3 fusion.19
  63.4 0.9 slice_add_fusion.20
  64.4 1.3 dynamic-slice
  66.4 0.2 dynamic-update-slice
  66.7 7.7 %all-reduce = f32[64]{0:T(128)S(1)} all-reduce(f32[64]{0:T(128)S(1)} %dynamic-update-slice), channel_id=2, replica_groups=mesh['seq_0'=16,'seq_1'=4,'head'=8] {'seq_1'}, use_global_device_ids=true, to_apply=%add | all-reduce | flops 64 | bytes 512
  74.3 0.1 fusion.56
  74.4 0.7 fusion.55
  75.1 30.7 %all-gather.6.cloned.1.call-done = f32[4,16,64,128]{3,2,1,0:T(8,128)} async-done(((f32[1,16,64,128]{3,2,1,0:T(8,128)}), f32[4,16,64,128]{3,2,1,0:T(8,128)}) %all-gather.6.cloned.1.call-update) | async-done | bytes 2097168 | tf_op jit(solution)/shard_map/all_gather | solution.py:33
  105.8 2.5 slice_add_fusion.16
  108.4 0.7 all-gather.10.cloned.1.call-update
  109.1 0.9 copy.86
  110.0 5.1 %all-to-all-start.4 = ((bf16[32,8,1024]{2,0,1:T(8,128)(2,1)}), bf16[32,8,1024]{2,0,1:T(8,128)(2,1)S(1)}, u32[]{:S(2)}, u32[]{:S(2)}) async-start(bf16[32,8,1024]{2,0,1:T(8,128)(2,1)} %bitcast.166), calls=%async_computation.4 | async-start | bytes 1048576 | tf_op jit(solution)/shard_map/all_to_all | solution.py:100
  115.1 0.6 iota_compare_fusion
  115.7 0.7 copy.62
  116.4 0.7 copy.60
  117.1 26.5 %all-gather.1 = f32[16,1,16]{2,1,0:T(1,128)S(1)} all-gather(f32[1,1,16]{2,1,0:T(1,128)S(1)} %get-tuple-element.7), channel_id=1, replica_groups=mesh['seq_0'=16,'seq_1'=4,'head'=8] {'seq_0'}, dimensions={0}, use_global_device_ids=true | all-gather | bytes 1088 | tf_op jit(solution)/shard_map/all_gather | solution.py:33
  143.6 0.6 fusion.54
  144.3 0.8 copy-done.2
  145.1 1.1 convert_bitcast_fusion
  146.2 1.7 reshape.345
  148.0 1.9 copy.71
  149.9 0.8 multiply_convert_fusion.5
  150.7 0.2 fusion.64
  150.9 3.1 convolution_bitcast_fusion.1
  153.9 60.6 %all-gather.8.cloned.1.call-done = f32[16,16,64,128]{3,2,1,0:T(8,128)} async-done(((f32[1,16,64,128]{3,2,1,0:T(8,128)}), f32[16,16,64,128]{3,2,1,0:T(8,128)}) %all-gather.8.cloned.1.call-update) | async-done | bytes 8388624 | tf_op jit(solution)/shard_map/all_gather | solution.py:33
  214.6 4.5 %fusion.60 = (bf16[1,16,64,128]{3,2,1,0:T(8,128)(2,1)S(1)}, f32[1,16,64,128]{3,2,1,0:T(8,128)S(1)}) fusion(pred[]{:T(512)S(6)} %gt.63, pred[]{:T(512)S(6)} %gt.62, f32[4,16,64,128]{3,2,1,0:T(8,128)S(1)} %copy-done.1, f32[16]{0:T(128)S(1)} %get-tuple-element.50, f32[16]{0:T(128)S(1)} %get-tuple-element.49, f32[16]{0:T(128)S(1)} %copy-done.12, pred[]{:T(512)S(6)} %gt.61, ...), kind=kLoop, calls=%fused_computation.164 | loop fusion | flops 7995392 | bytes 11273556 | tf_op jit(solution)/shard_map/convert_element_type | solution.py:155
  219.1 0.1 add_convert_fusion
  219.3 1.6 multiply_reduce_fusion
  220.9 2.2 copy.74
  223.1 1.6 reshape.435
  224.7 1.6 multiply_convert_fusion.2
  226.4 137.5 %all-gather.10.cloned.1.call-done = bf16[1024,4096]{0,1:T(8,128)(2,1)} async-done(((bf16[1024,64]{0,1:T(8,128)(2,1)}), bf16[1024,4096]{0,1:T(8,128)(2,1)}) %all-gather.10.cloned.1.call-update) | async-done | bytes 8388624 | tf_op jit(solution)/shard_map/all_gather | solution.py:172
  363.9 5.7 %convolution_convert_fusion = bf16[256,4096]{1,0:T(8,128)(2,1)S(1)} fusion(bf16[256,1024]{1,0:T(8,128)(2,1)S(1)} %multiply_convert_fusion.2, bf16[1024,4096]{0,1:T(8,128)(2,1)} %all-gather.10.cloned.1.call-done), kind=kOutput, calls=%fused_computation | convolution fusion | flops 2148532224 | bytes 11010048 | tf_op jit(solution)/shard_map/dot_general | solution.py:170
  369.6 38.7 %all_to_all.88 = bf16[8,32,4096]{2,1,0:T(8,128)(2,1)S(1)} all-to-all(bf16[8,32,4096]{2,1,0:T(8,128)(2,1)S(1)} %bitcast.172), channel_id=1, replica_groups=mesh['seq_0'=16,'seq_1'=4,'head'=8] {'head'}, dimensions={0} | all-to-all | bytes 4194304 | tf_op jit(solution)/shard_map/all_to_all | solution.py:51
  408.3 1.1 reduce_sum.32
  (58 shorter events, 0.4 us)
Async XLA Ops:
  6.5 11.6 %copy-start = (bf16[32,1024]{1,0:T(8,128)(2,1)S(1)}, bf16[32,1024]{1,0:T(8,128)(2,1)}, u32[]{:S(2)}) copy-start(bf16[32,1024]{1,0:T(8,128)(2,1)} %param.16) | copy-start | bytes 196612
  6.5 43.1 %copy-start.16 = (f32[16]{0:T(128)S(1)}, f32[16]{0:T(128)}, u32[]{:S(2)}) copy-start(f32[16]{0:T(128)} %param.19) | copy-start | bytes 196
  8.1 18.2 %all-to-all-start.3 = ((bf16[8,2,256]{2,1,0:T(2,128)(2,1)}), bf16[8,2,256]{2,1,0:T(2,128)(2,1)S(1)}, u32[]{:S(2)}, u32[]{:S(2)}) async-start(bf16[8,2,256]{2,1,0:T(2,128)(2,1)} %reshape.437), calls=%async_computation.3 | async-start | bytes 16384 | tf_op jit(solution)/shard_map/all_to_all | solution.py:103
  26.3 9.7 %all-to-all-start.1 = ((bf16[32,8,128]{2,0,1:T(8,128)(2,1)}), bf16[32,8,128]{2,0,1:T(8,128)(2,1)S(1)}, u32[]{:S(2)}, u32[]{:S(2)}) async-start(bf16[32,8,128]{2,0,1:T(8,128)(2,1)} %copy_bitcast_fusion.3), calls=%async_computation.1 | async-start | bytes 131072 | tf_op jit(solution)/shard_map/all_to_all | solution.py:101
  31.3 29.4 %copy-start.14 = (f32[1024]{0:T(1024)S(1)}, f32[1024]{0:T(1024)}, u32[]{:S(2)}) copy-start(f32[1024]{0:T(1024)} %param.23) | copy-start | bytes 12292
  36.0 8.9 %all-to-all-start.2 = ((bf16[32,8,128]{2,0,1:T(8,128)(2,1)}), bf16[32,8,128]{2,0,1:T(8,128)(2,1)S(1)}, u32[]{:S(2)}, u32[]{:S(2)}) async-start(bf16[32,8,128]{2,0,1:T(8,128)(2,1)} %copy_bitcast_fusion.2), calls=%async_computation.2 | async-start | bytes 131072 | tf_op jit(solution)/shard_map/all_to_all | solution.py:102
  44.9 13.6 %all-to-all-start = ((bf16[32,8,1024]{2,0,1:T(8,128)(2,1)}), bf16[32,8,1024]{2,0,1:T(8,128)(2,1)S(1)}, u32[]{:S(2)}, u32[]{:S(2)}) async-start(bf16[32,8,1024]{2,0,1:T(8,128)(2,1)} %bitcast.167), calls=%async_computation | async-start | bytes 1048576 | tf_op jit(solution)/shard_map/all_to_all | solution.py:99
  49.1 56.8 %all-gather.6.cloned.1.call-start = ((), (), s32[]{:S(2)}) async-start(), calls=%async_computation.6 | async-start | bytes 2621440 | tf_op jit(solution)/shard_map/all_gather | solution.py:33
  58.5 2.1 collective-permute-start
  62.9 1.4 copy-start.4
  64.4 44.7 %copy-start.7 = (bf16[32,8192]{1,0:T(8,128)(2,1)S(1)}, bf16[32,8192]{1,0:T(8,128)(2,1)}, u32[]{:S(2)}) copy-start(bf16[32,8192]{1,0:T(8,128)(2,1)} %param.15) | copy-start | bytes 1572868
  64.4 150.2 %all-gather.8.cloned.1.call-start = ((), (), s32[]{:S(2)}) async-start(), calls=%async_computation.7 | async-start | bytes 8912896 | tf_op jit(solution)/shard_map/all_gather | solution.py:33
  75.1 34.9 %copy-start.11 = (f32[16]{0:T(128)}, f32[16]{0:T(128)S(1)}, u32[]{:S(2)}) copy-start(f32[16]{0:T(128)S(1)} %get-tuple-element.52) | copy-start | bytes 196
  108.4 255.5 %all-gather.10.cloned.1.call-start = ((), (), s32[]{:S(2)}) async-start(), calls=%async_computation.8 | async-start | bytes 8519680 | tf_op jit(solution)/shard_map/all_gather | solution.py:172
  110.0 34.3 %all-to-all-start.4 = ((bf16[32,8,1024]{2,0,1:T(8,128)(2,1)}), bf16[32,8,1024]{2,0,1:T(8,128)(2,1)S(1)}, u32[]{:S(2)}, u32[]{:S(2)}) async-start(bf16[32,8,1024]{2,0,1:T(8,128)(2,1)} %bitcast.166), calls=%async_computation.4 | async-start | bytes 1048576 | tf_op jit(solution)/shard_map/all_to_all | solution.py:100
  144.3 0.8 copy-start.2
  147.9 2.9 copy-start.8
  147.9 2.9 copy-start.9
  147.9 2.9 copy-start.10
  150.6 63.9 %copy-start.1 = (f32[4,16,64,128]{3,2,1,0:T(8,128)S(1)}, f32[4,16,64,128]{3,2,1,0:T(8,128)}, u32[]{:S(2)}) copy-start(f32[4,16,64,128]{3,2,1,0:T(8,128)} %all-gather.6.cloned.1.call-done) | copy-start | bytes 6291460
  150.7 63.9 %copy-start.12 = (f32[16]{0:T(128)S(1)}, f32[16]{0:T(128)}, u32[]{:S(2)}) copy-start(f32[16]{0:T(128)} %copy-done.11) | copy-start | bytes 196
  214.6 4.6 %copy-start.15 = (f32[16]{0:T(128)S(1)}, f32[16]{0:T(128)}, u32[]{:S(2)}) copy-start(f32[16]{0:T(128)} %get-tuple-element.12) | copy-start | bytes 196
  214.6 4.7 %copy-start.5 = (bf16[2,128,16,64]{1,3,2,0:T(8,128)(2,1)S(1)}, bf16[2,128,16,64]{1,3,2,0:T(8,128)(2,1)}, u32[]{:S(2)}) copy-start(bf16[2,128,16,64]{1,3,2,0:T(8,128)(2,1)} %copy-done.4) | copy-start | bytes 1572868
  214.6 4.7 %copy-start.6 = (f32[2,128,16,64]{1,3,2,0:T(8,128)S(1)}, f32[2,128,16,64]{1,3,2,0:T(8,128)}, u32[]{:S(2)}) copy-start(f32[2,128,16,64]{1,3,2,0:T(8,128)} %copy.71) | copy-start | bytes 3145732
  214.6 4.7 %copy-start.17 = (f32[16]{0:T(128)S(1)}, f32[16]{0:T(128)}, u32[]{:S(2)}) copy-start(f32[16]{0:T(128)} %param.21) | copy-start | bytes 196
  214.6 4.7 %copy-start.18 = (f32[2,128,16,64]{1,3,2,0:T(8,128)S(1)}, f32[2,128,16,64]{1,3,2,0:T(8,128)}, u32[]{:S(2)}) copy-start(f32[2,128,16,64]{1,3,2,0:T(8,128)} %convolution_bitcast_fusion.1) | copy-start | bytes 3145732
  223.1 1.6 copy-start.3
  223.1 1.6 copy-start.13
Sparse Core Ops, SparseCore 0:
  64.5 41.2 all-gather.5
  108.5 106.0 all-gather.7
  217.5 146.3 all-gather.9
where the time goes:
time: 417 us; the launch traced here: 416 us
  waiting for transfers between devices  248 us (59%)
  blocking collectives  72.9 us (17%)
  starting transfers between devices  29.5 us (7%)
  local copies, waits for them, and re-layouts  23.4 us (6%)
  other arithmetic  17.4 us (4%)
  between operations  14.2 us (3%)
  matrix products  10.9 us (3%)
    all_gather x1, waiting for transfers between devices, per_device(): lax.all_gather(out_weight, SEQ, axis=1, tiled=True)  138 us
    all_gather x2, waiting for transfers between devices, entering(): pieces = jax.tree.map(lambda part: lax.all_gather(part, axis), total)  91.4 us
    all_to_all x1, blocking collectives, sent_and_summed(): pieces = lax.all_to_all(split_up(array, dim, count), axis, 0, 0, tiled=True)  38.7 us
    all_gather x1, blocking collectives, entering(): pieces = jax.tree.map(lambda part: lax.all_gather(part, axis), total)  26.5 us
    all_to_all x1, starting transfers between devices, per_device(): lax.all_to_all(dt_raw, 'head', split_axis=1, concat_axis=0, tiled=True)  10 us
    all_to_all x1, waiting for transfers between devices, per_device(): lax.all_to_all(x_proj, 'head', split_axis=1, concat_axis=0, tiled=True)  8.7 us
  transfers between devices with their start and end apart: 9, of which 7 were waited for; matrix products, arithmetic and copies ran while one was open for 9% of the time, Pallas kernels for 0%

commit v1 on v0

--- a/solution.py
+++ b/solution.py
@@ -11,6 +11,13 @@
 DI = 8192
 SEQ = ("seq_0", "seq_1")
 SEQ_HEAD = ("seq_0", "seq_1", "head")
+
+
+def gather_over(array, axis, along):
+    n_dev = lax.axis_size(axis)
+    blocks = jnp.stack([array for _ in range(n_dev)])
+    blocks = lax.all_to_all(blocks, axis, split_axis=0, concat_axis=0)
+    return jnp.concatenate(blocks, axis=along)
 
 
 def from_behind(array, axis, by):
@@ -167,11 +174,7 @@
     grouped = gated.reshape(token_count, -1, DI // GROUPS)
     normed = grouped / jnp.sqrt(jnp.mean(grouped * grouped, axis=-1, keepdims=True) + 1.0)
     normed = (normed.reshape(token_count, -1) * norm_weight).astype(jnp.bfloat16)
-    terms = jnp.dot(
-        normed,
-        lax.all_gather(out_weight, SEQ, axis=1, tiled=True),
-        preferred_element_type=jnp.float32,
-    )
+    terms = jnp.dot(normed, gather_over(out_weight, SEQ, 1), preferred_element_type=jnp.float32)
     mixed = sent_and_summed(terms.astype(jnp.bfloat16), "head", 0)
     return mixed.astype(jnp.bfloat16)
 

time: 417 us -> 649 us (1.56)
  blocking collectives: 72.9 us -> 419 us
  waiting for transfers between devices: 248 us -> 132 us
  starting transfers between devices: 29.5 us -> 39.7 us
    unnamed x1, blocking collectives: 7.68 us -> 351 us
    all_gather x1 -> x0, waiting for transfers between devices: 138 us -> none  [per_device(): lax.all_gather(out_weight, SEQ, axis=1, tiled=True)]
    all_gather x2, waiting for transfers between devices: 91.4 us -> 111 us  [entering(): pieces = jax.tree.map(lambda part: lax.all_gather(part, axis), total)]
    all_to_all x0 -> x1, blocking collectives: none -> 12.7 us  [per_device(): lax.all_to_all(z_proj, 'head', split_axis=1, concat_axis=0, tiled=True)]
    all_to_all x1, starting transfers between devices: 5.12 us -> 14.6 us  [gather_over(): blocks = lax.all_to_all(blocks, axis, split_axis=0, concat_axis=0)]
    all_to_all x1, blocking collectives: 38.7 us -> 31.1 us  [sent_and_summed(): pieces = lax.all_to_all(split_up(array, dim, count), axis, 0, 0, tiled=True)]
  transfers between devices with their start and end apart: 9 -> 8, of which waited for: 7 -> 7; matrix products, arithmetic and copies ran while one was open for 9% -> 5% of each run, Pallas kernels for 0% -> 0%
where the time goes in v1:
time: 649 us; the launch traced here: 648 us
  blocking collectives  419 us (65%)
  waiting for transfers between devices  132 us (20%)
  starting transfers between devices  39.7 us (6%)
  local copies, waits for them, and re-layouts  20.2 us (3%)
  between operations  14.6 us (2%)
  other arithmetic  12.6 us (2%)
  matrix products  10.2 us (2%)
    unnamed x1, blocking collectives  351 us
    all_gather x2, waiting for transfers between devices, entering(): pieces = jax.tree.map(lambda part: lax.all_gather(part, axis), total)  111 us
    all_to_all x1, blocking collectives, sent_and_summed(): pieces = lax.all_to_all(split_up(array, dim, count), axis, 0, 0, tiled=True)  31.1 us
    all_gather x1, blocking collectives, entering(): pieces = jax.tree.map(lambda part: lax.all_gather(part, axis), total)  24.1 us
    all_to_all x1, starting transfers between devices, gather_over(): blocks = lax.all_to_all(blocks, axis, split_axis=0, concat_axis=0)  14.6 us
  transfers between devices with their start and end apart: 8, of which 7 were waited for; matrix products, arithmetic and copies ran while one was open for 5% of the time, Pallas kernels for 0%

profile of v1, /device:TPU:1, one launch (start us, length us, event | category | flops | bytes accessed | tf_op | source)
XLA Modules:
  0.0 647.8 jit_solution(13853131028433914085)
XLA Ops:
  6.5 0.9 copy.63
  7.4 0.7 reshape.535
  8.1 10.1 %all-to-all-start.3 = ((bf16[8,2,256]{2,1,0:T(2,128)(2,1)}), bf16[8,2,256]{2,1,0:T(2,128)(2,1)S(1)}, u32[]{:S(2)}, u32[]{:S(2)}) async-start(bf16[8,2,256]{2,1,0:T(2,128)(2,1)} %reshape.535), calls=%async_computation.3 | async-start | bytes 16384 | tf_op jit(solution)/shard_map/all_to_all | solution.py:110
  18.2 0.6 copy_bitcast_fusion.3
  18.8 4.0 all-to-all-done.3
  22.8 4.0 all-to-all-start.1
  26.8 1.5 copy_bitcast_fusion.2
  28.3 3.4 all-to-all-done.1
  31.6 4.0 all-to-all-start.2
  35.7 1.9 copy.92
  37.6 3.0 all-to-all-done.2
  40.5 4.2 all-to-all-start
  44.8 9.3 %all-to-all-done = bf16[32,8,1024]{2,0,1:T(8,128)(2,1)S(1)} async-done(((bf16[32,8,1024]{2,0,1:T(8,128)(2,1)}), bf16[32,8,1024]{2,0,1:T(8,128)(2,1)S(1)}, u32[]{:S(2)}, u32[]{:S(2)}) %all-to-all-start) | async-done | bytes 524320 | tf_op jit(solution)/shard_map/all_to_all | solution.py:106
  54.1 12.7 %all_to_all.93 = bf16[32,8,1024]{2,0,1:T(8,128)(2,1)S(1)} all-to-all(bf16[32,8,1024]{2,0,1:T(8,128)(2,1)S(1)} %bitcast.164), channel_id=1, replica_groups=mesh['seq_0'=16,'seq_1'=4,'head'=8] {'head'}, dimensions={1} | all-to-all | bytes 1048576 | tf_op jit(solution)/shard_map/all_to_all | solution.py:107
  66.8 4.3 stack.5
  71.1 0.0 copy-start.11
  71.1 14.6 %all-to-all-start.5 = ((bf16[64,1024,64]{1,2,0:T(8,128)(2,1)}), bf16[64,1024,64]{1,2,0:T(8,128)(2,1)}, u32[]{:S(2)}, u32[]{:S(2)}) async-start(bf16[64,1024,64]{1,2,0:T(8,128)(2,1)} %stack.5), calls=%async_computation.5 | async-start | bytes 16777216 | tf_op jit(solution)/shard_map/all_to_all | solution.py:19
  85.7 0.0 all-gather.5.cloned.1.call-start
  85.9 0.1 reshape.536
  86.0 0.1 copy.64
  86.1 0.1 broadcast_multiply_fusion
  86.2 0.2 reduce_window_sum.11
  86.4 0.1 exponential_multiply_fusion
  86.6 2.8 collective-permute-start
  89.4 0.1 copy.70
  89.5 0.9 collective-permute-done
  90.4 0.1 maximum_convert_fusion
  90.6 0.7 multiply_convert_fusion.3
  91.2 0.7 reshape.534
  91.9 0.9 copy.68
  92.8 0.1 multiply_convert_fusion.5
  92.9 0.3 fusion.14
  93.2 0.9 slice_add_fusion.20
  94.2 0.0 all-gather.5.cloned.1.call-update
  94.2 0.0 all-gather.7.cloned.1.call-start
  94.2 1.3 dynamic-slice
  96.2 0.2 dynamic-update-slice
  96.4 351.0 %all-reduce = f32[64]{0:T(128)S(1)} all-reduce(f32[64]{0:T(128)S(1)} %dynamic-update-slice), channel_id=2, replica_groups=mesh['seq_0'=16,'seq_1'=4,'head'=8] {'seq_1'}, use_global_device_ids=true, to_apply=%add | all-reduce | flops 64 | bytes 512
  447.4 0.1 fusion.54
  447.5 0.1 fusion.53
  447.6 39.3 %all-gather.5.cloned.1.call-done = f32[4,16,64,128]{3,2,1,0:T(8,128)} async-done(((f32[1,16,64,128]{3,2,1,0:T(8,128)}), f32[4,16,64,128]{3,2,1,0:T(8,128)}) %all-gather.5.cloned.1.call-update) | async-done | bytes 2097168 | tf_op jit(solution)/shard_map/all_gather | solution.py:40
  486.9 2.5 slice_add_fusion.16
  489.4 0.0 all-gather.7.cloned.1.call-update
  489.5 0.1 copy.65
  489.5 0.1 copy.67
  489.6 0.1 copy.71
  489.7 24.1 %all-gather.1 = f32[16,1,16]{2,1,0:T(1,128)S(1)} all-gather(f32[1,1,16]{2,1,0:T(1,128)S(1)} %get-tuple-element.7), channel_id=1, replica_groups=mesh['seq_0'=16,'seq_1'=4,'head'=8] {'seq_0'}, dimensions={0}, use_global_device_ids=true | all-gather | bytes 1088 | tf_op jit(solution)/shard_map/all_gather | solution.py:40
  513.8 0.6 fusion.52
  514.4 1.2 convert_bitcast_fusion
  515.6 1.3 copy.75
  516.9 1.7 reshape.444
  518.6 1.9 copy.77
  520.5 0.1 multiply_convert_fusion.6
  520.7 0.2 fusion.63
  520.8 3.1 convolution_bitcast_fusion.1
  523.9 71.7 %all-gather.7.cloned.1.call-done = f32[16,16,64,128]{3,2,1,0:T(8,128)} async-done(((f32[1,16,64,128]{3,2,1,0:T(8,128)}), f32[16,16,64,128]{3,2,1,0:T(8,128)}) %all-gather.7.cloned.1.call-update) | async-done | bytes 8388624 | tf_op jit(solution)/shard_map/all_gather | solution.py:40
  595.7 4.5 fusion.59
  600.2 0.1 add_convert_fusion
  600.4 0.6 multiply_reduce_fusion
  601.0 0.8 copy.72
  601.8 0.8 reshape.437
  602.7 6.0 convolution_convert_fusion
  608.8 31.1 %all_to_all.94 = bf16[8,32,4096]{2,1,0:T(8,128)(2,1)S(1)} all-to-all(bf16[8,32,4096]{2,1,0:T(8,128)(2,1)S(1)} %bitcast.163), channel_id=1, replica_groups=mesh['seq_0'=16,'seq_1'=4,'head'=8] {'head'}, dimensions={0} | all-to-all | bytes 4194304 | tf_op jit(solution)/shard_map/all_to_all | solution.py:58
  639.9 1.1 reduce_sum.32
  (69 shorter events, 0.3 us)
Async XLA Ops:
  6.5 11.7 %copy-start = (bf16[32,1024]{1,0:T(8,128)(2,1)S(1)}, bf16[32,1024]{1,0:T(8,128)(2,1)}, u32[]{:S(2)}) copy-start(bf16[32,1024]{1,0:T(8,128)(2,1)} %param.16) | copy-start | bytes 196612
  6.5 38.2 %copy-start.6 = (bf16[32,8192]{1,0:T(8,128)(2,1)S(1)}, bf16[32,8192]{1,0:T(8,128)(2,1)}, u32[]{:S(2)}) copy-start(bf16[32,8192]{1,0:T(8,128)(2,1)} %param.15) | copy-start | bytes 1572868
  8.1 14.7 %all-to-all-start.3 = ((bf16[8,2,256]{2,1,0:T(2,128)(2,1)}), bf16[8,2,256]{2,1,0:T(2,128)(2,1)S(1)}, u32[]{:S(2)}, u32[]{:S(2)}) async-start(bf16[8,2,256]{2,1,0:T(2,128)(2,1)} %reshape.535), calls=%async_computation.3 | async-start | bytes 16384 | tf_op jit(solution)/shard_map/all_to_all | solution.py:110
  22.8 8.8 %all-to-all-start.1 = ((bf16[32,8,128]{2,0,1:T(8,128)(2,1)}), bf16[32,8,128]{2,0,1:T(8,128)(2,1)S(1)}, u32[]{:S(2)}, u32[]{:S(2)}) async-start(bf16[32,8,128]{2,0,1:T(8,128)(2,1)} %copy_bitcast_fusion.3), calls=%async_computation.1 | async-start | bytes 131072 | tf_op jit(solution)/shard_map/all_to_all | solution.py:108
  31.6 8.9 %all-to-all-start.2 = ((bf16[32,8,128]{2,0,1:T(8,128)(2,1)}), bf16[32,8,128]{2,0,1:T(8,128)(2,1)S(1)}, u32[]{:S(2)}, u32[]{:S(2)}) async-start(bf16[32,8,128]{2,0,1:T(8,128)(2,1)} %copy_bitcast_fusion.2), calls=%async_computation.2 | async-start | bytes 131072 | tf_op jit(solution)/shard_map/all_to_all | solution.py:109
  35.7 31.1 %copy-start.7 = (bf16[1024,64]{0,1:T(8,128)(2,1)S(1)}, bf16[1024,64]{0,1:T(8,128)(2,1)}, u32[]{:S(2)}) copy-start(bf16[1024,64]{0,1:T(8,128)(2,1)} %param.27) | copy-start | bytes 393220
  40.5 13.6 %all-to-all-start = ((bf16[32,8,1024]{2,0,1:T(8,128)(2,1)}), bf16[32,8,1024]{2,0,1:T(8,128)(2,1)S(1)}, u32[]{:S(2)}, u32[]{:S(2)}) async-start(bf16[32,8,1024]{2,0,1:T(8,128)(2,1)} %bitcast.157), calls=%async_computation | async-start | bytes 1048576 | tf_op jit(solution)/shard_map/all_to_all | solution.py:106
  71.1 14.6 %copy-start.22 = (f32[16]{0:T(128)S(1)}, f32[16]{0:T(128)}, u32[]{:S(2)}) copy-start(f32[16]{0:T(128)} %param.20) | copy-start | bytes 196
  71.1 14.7 %copy-start.20 = (f32[2,128]{1,0:T(2,128)S(1)}, f32[2,128]{1,0:T(2,128)}, u32[]{:S(2)}) copy-start(f32[2,128]{1,0:T(2,128)} %param.25) | copy-start | bytes 3076
  71.1 14.7 %copy-start.9 = (f32[4,2,128]{2,1,0:T(2,128)S(1)}, f32[4,2,128]{2,1,0:T(2,128)}, u32[]{:S(2)}) copy-start(f32[4,2,128]{2,1,0:T(2,128)} %param.24) | copy-start | bytes 12292
  71.1 14.7 %copy-start.8 = (f32[4,1024]{1,0:T(4,128)S(1)}, f32[4,1024]{1,0:T(4,128)}, u32[]{:S(2)}) copy-start(f32[4,1024]{1,0:T(4,128)} %param.22) | copy-start | bytes 49156
  71.1 14.9 %copy-start.11 = (f32[16]{0:T(128)S(1)}, f32[16]{0:T(128)}, u32[]{:S(2)}) copy-start(f32[16]{0:T(128)} %param.19) | copy-start | bytes 196
  71.1 531.6 %all-to-all-start.5 = ((bf16[64,1024,64]{1,2,0:T(8,128)(2,1)}), bf16[64,1024,64]{1,2,0:T(8,128)(2,1)}, u32[]{:S(2)}, u32[]{:S(2)}) async-start(bf16[64,1024,64]{1,2,0:T(8,128)(2,1)} %stack.5), calls=%async_computation.5 | async-start | bytes 16777216 | tf_op jit(solution)/shard_map/all_to_all | solution.py:19
  85.7 4.9 copy-start.10
  85.7 401.2 %all-gather.5.cloned.1.call-start = ((), (), s32[]{:S(2)}) async-start(), calls=%async_computation.7 | async-start | bytes 2621440 | tf_op jit(solution)/shard_map/all_gather | solution.py:40
  86.6 3.8 collective-permute-start
  92.8 1.4 copy-start.2
  94.2 501.4 %all-gather.7.cloned.1.call-start = ((), (), s32[]{:S(2)}) async-start(), calls=%async_computation.8 | async-start | bytes 8912896 | tf_op jit(solution)/shard_map/all_gather | solution.py:40
  520.6 75.0 %copy-start.1 = (f32[4,16,64,128]{3,2,1,0:T(8,128)S(1)}, f32[4,16,64,128]{3,2,1,0:T(8,128)}, u32[]{:S(2)}) copy-start(f32[4,16,64,128]{3,2,1,0:T(8,128)} %all-gather.5.cloned.1.call-done) | copy-start | bytes 6291460
  520.6 75.0 %copy-start.12 = (f32[16]{0:T(128)S(1)}, f32[16]{0:T(128)}, u32[]{:S(2)}) copy-start(f32[16]{0:T(128)} %get-tuple-element.32) | copy-start | bytes 196
  520.6 75.0 %copy-start.13 = (f32[16]{0:T(128)S(1)}, f32[16]{0:T(128)}, u32[]{:S(2)}) copy-start(f32[16]{0:T(128)} %get-tuple-element.33) | copy-start | bytes 196
  520.6 75.0 %copy-start.14 = (f32[16]{0:T(128)S(1)}, f32[16]{0:T(128)}, u32[]{:S(2)}) copy-start(f32[16]{0:T(128)} %get-tuple-element.34) | copy-start | bytes 196
  520.6 75.0 %copy-start.15 = (f32[16]{0:T(128)S(1)}, f32[16]{0:T(128)}, u32[]{:S(2)}) copy-start(f32[16]{0:T(128)} %get-tuple-element.35) | copy-start | bytes 196
  520.6 75.0 %copy-start.16 = (f32[16]{0:T(128)S(1)}, f32[16]{0:T(128)}, u32[]{:S(2)}) copy-start(f32[16]{0:T(128)} %get-tuple-element.36) | copy-start | bytes 196
  520.6 75.0 %copy-start.17 = (f32[16]{0:T(128)S(1)}, f32[16]{0:T(128)}, u32[]{:S(2)}) copy-start(f32[16]{0:T(128)} %get-tuple-element.37) | copy-start | bytes 196
  520.6 75.0 %copy-start.18 = (f32[16]{0:T(128)S(1)}, f32[16]{0:T(128)}, u32[]{:S(2)}) copy-start(f32[16]{0:T(128)} %get-tuple-element.38) | copy-start | bytes 196
  520.7 75.0 %copy-start.19 = (f32[16]{0:T(128)S(1)}, f32[16]{0:T(128)}, u32[]{:S(2)}) copy-start(f32[16]{0:T(128)} %get-tuple-element.39) | copy-start | bytes 196
  595.7 4.7 copy-start.3
  595.7 4.7 copy-start.4
  595.7 4.7 copy-start.23
  595.7 4.7 copy-start.24
  601.0 1.7 copy-start.5
  601.0 1.7 copy-start.21
Sparse Core Ops, SparseCore 0:
  94.3 392.5 all-gather.4
  489.6 105.9 all-gather.6
